TPU v7x, 512 devices: a 4x2x32 block of a 4x16x32 slice. The times are simulated.
512 devices in a mesh: group: 2 (over y), expert: 32 (over z), tensor: 4 (over x), sub: 2 (over core).
Axes of the slice: x: 4, y: 2, z: 32, core: 2. Of those that a mesh axis runs over, the one named last changes fastest.
The devices are a block of a 4x16x32 slice.
Arguments:
- tokens: bfloat16 [512, 7168], P(('group', 'expert', 'sub')), parts along dimension 0, may hold values from -6 to 6
- expert_ids: int32 [512, 8], P(('group', 'expert', 'sub')), parts along dimension 0, may hold values from 0 to 15, all different within a row; in each aligned block of 4 rows (0 to 3, 4 to 7, ...) at most 3 rows name the same one
- gate_codes: int32 [512, 8], P(('group', 'expert', 'sub')), parts along dimension 0, may hold values from 1 to 63
- w_gate: bfloat16 [32, 1024, 7168], P('expert', ('tensor', 'sub')), may hold values from -0.0625 to 0.0625
- w_up: bfloat16 [32, 1024, 7168], P('expert', ('tensor', 'sub')), may hold values from -0.0625 to 0.0625
- w_down: bfloat16 [32, 1024, 7168], P('expert', ('tensor', 'sub')), may hold values from -0.125 to 0.125
Outputs:
- mixed: bfloat16 [512, 7168], P(('group', 'expert', 'sub'), 'tensor'), parts along dimension 0
There are 2 independent parts, one for each index of `group`. A program takes and returns all parts, laid end to end along the dimension named above; an argument that names none is the same for every part. Nothing has to cross between parts.
Inputs may be any that keep to these rules, and one draw needn't show every extreme that they name: `expert_ids`: the 8 numbers of a row differ; within the rows of one device (aligned blocks of 4 rows) no expert is named by more than 3 rows, a bound that some block reaches.
All inputs are finite; a program needn't handle non-finite values.
Results may differ from a plain program's by a relative error of at most 0.008.
Values may be sent and summed in bfloat16 or wider, within the bound.
A program may use at most 64 MiB of HBM per device.

v0:
```python
import jax
import jax.numpy as jnp
from jax import lax
from jax.sharding import PartitionSpec as P


def shards(tokens, expert_ids, gate_codes, w_gate, w_up, w_down):
    tok_rows, features = tokens.shape
    per_token = expert_ids.shape[1]
    owners = lax.axis_size("expert")
    sub_count = lax.axis_size("sub")
    tensor_count = lax.axis_size("tensor")
    experts = owners // 2
    capacity = min(tok_rows, tok_rows * per_token // experts + 1)
    flat_ids = expert_ids.reshape(-1)
    matches = (flat_ids[:, None] == jnp.arange(experts, dtype=jnp.int32)[None, :]).astype(jnp.int32)
    before = jnp.cumsum(matches, axis=0) - matches
    slot_index = jnp.sum(before * matches, axis=1)
    position = flat_ids * capacity + slot_index
    onehot = position[:, None] == jnp.arange(experts * capacity, dtype=jnp.int32)[None, :]
    weights = gate_codes.reshape(-1).astype(jnp.float32) / 64.0
    choose = jnp.any(onehot.reshape(tok_rows, per_token, -1), axis=1).astype(jnp.bfloat16)
    combine = jnp.sum(
        jnp.where(onehot, weights[:, None], 0.0).reshape(tok_rows, per_token, -1), axis=1
    )
    packed = jnp.dot(choose.T, tokens, preferred_element_type=jnp.float32).astype(jnp.bfloat16)
    outgoing = jnp.broadcast_to(
        packed.reshape(experts, 1, capacity, features), (experts, 2, capacity, features)
    )
    arrived = lax.all_to_all(
        outgoing.reshape(owners, capacity, features),
        "expert",
        split_axis=0,
        concat_axis=0,
        tiled=True,
    )
    slot_rows = lax.all_gather(arrived, "sub", axis=1, tiled=True).reshape(-1, features)
    contract = (((1,), (1,)), ((), ()))
    gate_act = lax.dot_general(slot_rows, w_gate[0], contract, preferred_element_type=jnp.float32)
    up_act = lax.dot_general(slot_rows, w_up[0], contract, preferred_element_type=jnp.float32)
    hidden = (jax.nn.silu(gate_act) * up_act).astype(jnp.bfloat16)
    partial_value = jnp.dot(hidden, w_down[0], preferred_element_type=jnp.float32).astype(
        jnp.bfloat16
    )
    partial_value = partial_value.reshape(owners, sub_count, capacity, features)
    block = features // tensor_count
    sectioned = partial_value.reshape(owners, sub_count, capacity, tensor_count, block).transpose(
        0, 2, 3, 1, 4
    )
    sectioned = sectioned.reshape(owners, capacity, tensor_count * sub_count, block)
    gathered = lax.all_to_all(sectioned, ("tensor", "sub"), split_axis=2, concat_axis=2, tiled=True)
    run_total = jnp.sum(gathered.astype(jnp.float32), axis=2)
    came_back = lax.all_to_all(
        run_total.astype(jnp.bfloat16), "expert", split_axis=0, concat_axis=0, tiled=True
    ).astype(run_total.dtype)
    summed = jnp.sum(came_back.reshape(experts, 2, capacity, block), axis=1)
    mixed = jnp.dot(
        combine,
        summed.reshape(-1, block),
        precision=lax.Precision.HIGHEST,
        preferred_element_type=jnp.float32,
    )
    return mixed.astype(jnp.bfloat16)


def solution(mesh):
    return jax.shard_map(
        shards,
        mesh=mesh,
        in_specs=(
            P(("group", "expert", "sub"), None),
            P(("group", "expert", "sub"), None),
            P(("group", "expert", "sub"), None),
            P("expert", ("tensor", "sub"), None),
            P("expert", ("tensor", "sub"), None),
            P("expert", ("tensor", "sub"), None),
        ),
        out_specs=P(("group", "expert", "sub"), "tensor"),
        check_vma=False,
    )
```

profile of v0, /device:TPU:40, one launch (start us, length us, event | category | flops | bytes accessed | tf_op | source)
XLA Modules:
  0.0 407.4 jit_solution(4467936220724837105)
XLA Ops:
  6.5 0.0 copy-start
  6.6 0.0 all-gather.2.cloned.1.call-start
  6.6 0.9 eq.30
  7.4 0.1 fusion.20
  7.5 0.1 reduce_window_sum.11
  7.6 0.2 select_reduce_fusion.1
  7.8 0.1 reduce_sum.42
  7.8 0.7 multiply_add_fusion
  8.5 0.1 fusion.19
  8.6 1.2 convolution_convert_fusion.1
  9.8 0.4 broadcast_in_dim.25
  10.3 0.5 broadcast_in_dim.26
  10.8 221.8 %all_to_all.15 = bf16[32,3,7168]{2,1,0:T(4,128)(2,1)S(1)} all-to-all(bf16[32,3,7168]{2,1,0:T(4,128)(2,1)S(1)} %bitcast.29), channel_id=1, replica_groups=mesh['group'=2,'expert'=32,'tensor'=4,'sub'=2] {'expert'}, dimensions={0} | all-to-all | bytes 2752512 | tf_op jit(solution)/shard_map/all_to_all | solution.py:30
  232.6 1.6 copy.21
  234.2 0.1 all-gather.2.cloned.1.call-update
  234.3 12.8 %all-gather.2.cloned.1.call-done = bf16[32,6,7168]{2,0,1:T(8,128)(2,1)} async-done(((bf16[32,3,7168]{2,0,1:T(8,128)(2,1)}), bf16[32,6,7168]{2,0,1:T(8,128)(2,1)}) %all-gather.2.cloned.1.call-update) | async-done | bytes 2752528 | tf_op jit(solution)/shard_map/all_gather | solution.py:37
  247.1 5.1 %copy.22 = bf16[32,6,7168]{2,1,0:T(8,128)(2,1)} copy(bf16[32,6,7168]{2,0,1:T(8,128)(2,1)} %all-gather.2.cloned.1.call-done) | data formatting | bytes 5505024 | tf_op jit(solution)/shard_map/all_gather | solution.py:37
  252.2 4.6 %reshape.60 = bf16[192,7168]{1,0:T(8,128)(2,1)} reshape(bf16[32,6,7168]{2,1,0:T(8,128)(2,1)} %copy.22) | data formatting | bytes 5505024 | tf_op jit(solution)/shard_map/reshape | solution.py:37
  256.9 3.2 fusion.3
  260.1 0.0 copy-done
  260.1 7.0 %convolution_convert_fusion = bf16[192,7168]{1,0:T(8,128)(2,1)} fusion(bf16[1,128,7168]{2,1,0:T(8,128)(2,1)S(1)} %copy-done, bf16[192,7168]{1,0:T(8,128)(2,1)} %reshape.60, bf16[1,128,7168]{2,1,0:T(8,128)(2,1)} %param.10, f32[192,128]{1,0:T(8,128)S(1)} %fusion.3), kind=kOutput, calls=%fused_computation | convolution fusion | flops 706166784 | bytes 9273344 | tf_op jit(solution)/shard_map/dot_general | solution.py:42
  267.0 6.2 %reshape_reshape.3 = bf16[32,2,3,4,1792]{4,3,2,1,0:T(4,128)(2,1)} reshape(bf16[192,7168]{1,0:T(8,128)(2,1)} %convolution_convert_fusion) | data formatting | bytes 5505024 | tf_op jit(solution)/shard_map/reshape;reshape | solution.py:47
  273.3 2.3 copy.29
  275.6 38.4 %all_to_all.16 = bf16[32,3,8,1792]{3,0,1,2:T(8,128)(2,1)} all-to-all(bf16[32,3,8,1792]{3,0,1,2:T(8,128)(2,1)S(1)} %bitcast.28), channel_id=1, replica_groups=mesh['group'=2,'expert'=32,'tensor'=4,'sub'=2] {'tensor','sub'}, dimensions={2} | all-to-all | bytes 5505024 | tf_op jit(solution)/shard_map/all_to_all | solution.py:51
  314.0 0.0 copy-start.1
  314.0 2.2 reduce_sum.44
  316.2 1.1 copy.26
  317.3 23.3 %all-to-all-start.2 = ((bf16[32,3,1792]{2,1,0:T(4,128)(2,1)}), bf16[32,3,1792]{2,1,0:T(4,128)(2,1)S(1)}, u32[]{:S(2)}, u32[]{:S(2)}) async-start(bf16[32,3,1792]{2,1,0:T(4,128)(2,1)} %copy.26), calls=%async_computation.2 | async-start | bytes 917504 | tf_op jit(solution)/shard_map/all_to_all | solution.py:53
  340.6 0.0 copy-done.1
  340.7 0.1 select_reduce_fusion
  340.7 58.5 %all-to-all-done.2 = bf16[32,3,1792]{2,1,0:T(4,128)(2,1)S(1)} async-done(((bf16[32,3,1792]{2,1,0:T(4,128)(2,1)}), bf16[32,3,1792]{2,1,0:T(4,128)(2,1)S(1)}, u32[]{:S(2)}, u32[]{:S(2)}) %all-to-all-start.2) | async-done | bytes 344096 | tf_op jit(solution)/shard_map/all_to_all | solution.py:53
  399.2 0.3 convert_reduce_fusion
  399.5 0.2 reshape.64
  399.6 0.9 convolution_convert_fusion.2
  (1 shorter events, 0.0 us)
Async XLA Ops:
  6.5 253.5 %copy-start = (bf16[1,128,7168]{2,1,0:T(8,128)(2,1)S(1)}, bf16[1,128,7168]{2,1,0:T(8,128)(2,1)}, u32[]{:S(2)}) copy-start(bf16[1,128,7168]{2,1,0:T(8,128)(2,1)} %param.11) | copy-start | bytes 5505028
  6.6 240.6 %all-gather.2.cloned.1.call-start = ((), (), s32[]{:S(2)}) async-start(), calls=%async_computation.3 | async-start | bytes 4128768 | tf_op jit(solution)/shard_map/all_gather | solution.py:37
  314.0 26.6 %copy-start.1 = (s32[4,8]{1,0:T(4,128)S(1)}, s32[4,8]{1,0:T(4,128)}, u32[]{:S(2)}) copy-start(s32[4,8]{1,0:T(4,128)} %param.8) | copy-start | bytes 388
  317.3 81.9 %all-to-all-start.2 = ((bf16[32,3,1792]{2,1,0:T(4,128)(2,1)}), bf16[32,3,1792]{2,1,0:T(4,128)(2,1)S(1)}, u32[]{:S(2)}, u32[]{:S(2)}) async-start(bf16[32,3,1792]{2,1,0:T(4,128)(2,1)} %copy.26), calls=%async_computation.2 | async-start | bytes 917504 | tf_op jit(solution)/shard_map/all_to_all | solution.py:53
Sparse Core Ops, SparseCore 0:
  234.4 12.6 all-gather.1
where the time goes:
time: 408 us; the launch traced here: 407 us
  blocking collectives  260 us (64%)
  waiting for transfers between devices  71.3 us (17%)
  starting transfers between devices  23.3 us (6%)
  local copies, waits for them, and re-layouts  23.1 us (6%)
  between operations  13.5 us (3%)
  matrix products  12.2 us (3%)
    all_to_all x1, blocking collectives, shards(): lax.all_to_all(outgoing.reshape(owners, capacity, features), 'expert', sp...  222 us
    all_to_all x1, waiting for transfers between devices, shards(): lax.all_to_all(run_total.astype(jnp.bfloat16), 'expert', split_axis=0, co...  58.5 us
    all_to_all x1, blocking collectives, shards(): lax.all_to_all(sectioned, ('tensor', 'sub'), split_axis=2, concat_axis=2,...  38.4 us
    all_to_all x1, starting transfers between devices, shards(): lax.all_to_all(run_total.astype(jnp.bfloat16), 'expert', split_axis=0, co...  23.3 us
    all_gather x1, waiting for transfers between devices, shards(): lax.all_gather(arrived, 'sub', axis=1, tiled=True).reshape(-1, features)  12.8 us
  transfers between devices with their start and end apart: 2, of which 2 were waited for; matrix products, arithmetic and copies ran while one was open for 0% of the time, Pallas kernels for 0%

commit v1 on v0

--- a/solution.py
+++ b/solution.py
@@ -34,7 +34,9 @@
         concat_axis=0,
         tiled=True,
     )
-    slot_rows = lax.all_gather(arrived, "sub", axis=1, tiled=True).reshape(-1, features)
+    slot_rows = jnp.concatenate(
+        lax.all_to_all(jnp.stack([arrived] * lax.axis_size("sub")), "sub", 0, 0), axis=1
+    ).reshape(-1, features)
     contract = (((1,), (1,)), ((), ()))
     gate_act = lax.dot_general(slot_rows, w_gate[0], contract, preferred_element_type=jnp.float32)
     up_act = lax.dot_general(slot_rows, w_up[0], contract, preferred_element_type=jnp.float32)

time: 408 us -> 373 us (0.914)
  starting transfers between devices: 23.3 us -> 4.8 us
  between operations: 13.5 us -> 0.1 us
  waiting for transfers between devices: 71.3 us -> 58.8 us
  blocking collectives: 260 us -> 266 us
    all_to_all x1, starting transfers between devices: 23.3 us -> 4.8 us  [shards(): lax.all_to_all(run_total.astype(jnp.bfloat16), 'expert', split_axis=0, co...]
    all_gather x1 -> x0, waiting for transfers between devices: 12.8 us -> none  [shards(): lax.all_gather(arrived, 'sub', axis=1, tiled=True).reshape(-1, features)]
    another operation x0 -> x2, local copies, waits for them, and re-layouts: none -> 8.13 us  [the longest x1 7.07 us: shards(): slot_rows = jnp.concatenate(lax.all_to_all(jnp.stack([arrived] * lax.axis...]
    all_to_all x0 -> x1, blocking collectives: none -> 5.96 us  [shards(): lax.all_to_all(jnp.stack([arrived] * lax.axis_size('sub')), 'sub', 0, 0)]
    all_gather x1 -> x0, local copies, waits for them, and re-layouts: 5.11 us -> none  [shards(): lax.all_gather(arrived, 'sub', axis=1, tiled=True).reshape(-1, features)]
  transfers between devices with their start and end apart: 2 -> 1, of which waited for: 2 -> 1; matrix products, arithmetic and copies ran while one was open for 0% -> 0% of each run, Pallas kernels for 0% -> 0%
where the time goes in v1:
time: 373 us; the launch traced here: 372 us
  blocking collectives  266 us (71%)
  waiting for transfers between devices  58.8 us (16%)
  local copies, waits for them, and re-layouts  24 us (6%)
  matrix products  12.2 us (3%)
  other arithmetic  5.34 us (1%)
  starting transfers between devices  4.8 us (1%)
    all_to_all x1, blocking collectives, shards(): lax.all_to_all(outgoing.reshape(owners, capacity, features), 'expert', sp...  222 us
    all_to_all x1, waiting for transfers between devices, shards(): lax.all_to_all(run_total.astype(jnp.bfloat16), 'expert', split_axis=0, co...  58.8 us
    all_to_all x1, blocking collectives, shards(): lax.all_to_all(sectioned, ('tensor', 'sub'), split_axis=2, concat_axis=2,...  38.7 us
  transfers between devices with their start and end apart: 1, of which 1 were waited for; matrix products, arithmetic and copies ran while one was open for 0% of the time, Pallas kernels for 0%

profile of v1, /device:TPU:40, one launch (start us, length us, event | category | flops | bytes accessed | tf_op | source)
XLA Modules:
  0.0 371.8 jit_solution(7873419184703963555)
XLA Ops:
  0.0 0.0 copy-start
  0.0 0.9 eq.30
  0.9 0.1 fusion.20
  1.0 0.1 reduce_window_sum.11
  1.0 0.2 select_reduce_fusion.1
  1.2 0.1 reduce_sum.42
  1.3 0.7 multiply_add_fusion
  2.0 0.1 fusion.19
  2.1 1.2 convolution_convert_fusion.1
  3.3 0.4 broadcast_in_dim.25
  3.8 0.5 broadcast_in_dim.26
  4.3 221.8 %all_to_all.20 = bf16[32,3,7168]{2,1,0:T(4,128)(2,1)S(1)} all-to-all(bf16[32,3,7168]{2,1,0:T(4,128)(2,1)S(1)} %bitcast.32), channel_id=1, replica_groups=mesh['group'=2,'expert'=32,'tensor'=4,'sub'=2] {'expert'}, dimensions={0} | all-to-all | bytes 2752512 | tf_op jit(solution)/shard_map/all_to_all | solution.py:30
  226.1 1.7 pad_maximum_fusion
  227.8 1.1 copy.21
  228.8 6.0 %all_to_all.21 = bf16[2,32,3,7168]{3,1,2,0:T(8,128)(2,1)S(1)} all-to-all(bf16[2,32,3,7168]{3,1,2,0:T(8,128)(2,1)S(1)} %copy.21), channel_id=1, replica_groups=mesh['group'=2,'expert'=32,'tensor'=4,'sub'=2] {'sub'}, dimensions={0} | all-to-all | bytes 5505024 | tf_op jit(solution)/shard_map/all_to_all | solution.py:38
  234.8 4.2 %copy.22 = bf16[32,2,3,7168]{3,2,1,0:T(4,128)(2,1)} copy(bf16[32,2,3,7168]{3,0,2,1:T(8,128)(2,1)S(1)} %bitcast.30) | data formatting | bytes 5505024 | tf_op jit(solution)/shard_map/reshape | solution.py:37
  238.9 7.1 %reshape_reshape.6 = bf16[192,7168]{1,0:T(8,128)(2,1)} reshape(bf16[32,2,3,7168]{3,2,1,0:T(4,128)(2,1)} %copy.22) | data formatting | bytes 5505024 | tf_op jit(solution)/shard_map/reshape;reshape | solution.py:39
  246.0 3.2 fusion.3
  249.2 0.0 copy-done
  249.2 7.0 %convolution_convert_fusion = bf16[192,7168]{1,0:T(8,128)(2,1)} fusion(bf16[1,128,7168]{2,1,0:T(8,128)(2,1)S(1)} %copy-done, bf16[192,7168]{1,0:T(8,128)(2,1)} %reshape_reshape.6, bf16[1,128,7168]{2,1,0:T(8,128)(2,1)} %param.10, f32[192,128]{1,0:T(8,128)S(1)} %fusion.3), kind=kOutput, calls=%fused_computation | convolution fusion | flops 706166784 | bytes 9273344 | tf_op jit(solution)/shard_map/dot_general | solution.py:44
  256.2 6.2 %reshape_reshape.7 = bf16[32,2,3,4,1792]{4,3,2,1,0:T(4,128)(2,1)} reshape(bf16[192,7168]{1,0:T(8,128)(2,1)} %convolution_convert_fusion) | data formatting | bytes 5505024 | tf_op jit(solution)/shard_map/reshape;reshape | solution.py:49
  262.4 2.3 copy.29
  264.7 38.7 %all_to_all.22 = bf16[32,3,8,1792]{3,0,1,2:T(8,128)(2,1)} all-to-all(bf16[32,3,8,1792]{3,0,1,2:T(8,128)(2,1)S(1)} %bitcast.31), channel_id=1, replica_groups=mesh['group'=2,'expert'=32,'tensor'=4,'sub'=2] {'tensor','sub'}, dimensions={2} | all-to-all | bytes 5505024 | tf_op jit(solution)/shard_map/all_to_all | solution.py:53
  303.5 0.0 copy-start.1
  303.5 2.2 reduce_sum.44
  305.7 1.1 copy.26
  306.8 4.8 %all-to-all-start.3 = ((bf16[32,3,1792]{2,1,0:T(4,128)(2,1)}), bf16[32,3,1792]{2,1,0:T(4,128)(2,1)S(1)}, u32[]{:S(2)}, u32[]{:S(2)}) async-start(bf16[32,3,1792]{2,1,0:T(4,128)(2,1)} %copy.26), calls=%async_computation.3 | async-start | bytes 917504 | tf_op jit(solution)/shard_map/all_to_all | solution.py:55
  311.6 0.0 copy-done.1
  311.6 0.1 select_reduce_fusion
  311.7 58.8 %all-to-all-done.3 = bf16[32,3,1792]{2,1,0:T(4,128)(2,1)S(1)} async-done(((bf16[32,3,1792]{2,1,0:T(4,128)(2,1)}), bf16[32,3,1792]{2,1,0:T(4,128)(2,1)S(1)}, u32[]{:S(2)}, u32[]{:S(2)}) %all-to-all-start.3) | async-done | bytes 344096 | tf_op jit(solution)/shard_map/all_to_all | solution.py:55
  370.5 0.3 convert_reduce_fusion
  370.8 0.2 reshape.64
  370.9 0.9 convolution_convert_fusion.2
  (1 shorter events, 0.0 us)
Async XLA Ops:
  0.0 249.2 %copy-start = (bf16[1,128,7168]{2,1,0:T(8,128)(2,1)S(1)}, bf16[1,128,7168]{2,1,0:T(8,128)(2,1)}, u32[]{:S(2)}) copy-start(bf16[1,128,7168]{2,1,0:T(8,128)(2,1)} %param.11) | copy-start | bytes 5505028
  303.5 8.1 %copy-start.1 = (s32[4,8]{1,0:T(4,128)S(1)}, s32[4,8]{1,0:T(4,128)}, u32[]{:S(2)}) copy-start(s32[4,8]{1,0:T(4,128)} %param.8) | copy-start | bytes 388
  306.8 63.7 %all-to-all-start.3 = ((bf16[32,3,1792]{2,1,0:T(4,128)(2,1)}), bf16[32,3,1792]{2,1,0:T(4,128)(2,1)S(1)}, u32[]{:S(2)}, u32[]{:S(2)}) async-start(bf16[32,3,1792]{2,1,0:T(4,128)(2,1)} %copy.26), calls=%async_computation.3 | async-start | bytes 917504 | tf_op jit(solution)/shard_map/all_to_all | solution.py:55
